TPU v7x, 32 devices: a whole 2x2x4 slice. The times are simulated.
32 devices in a mesh: gx: 4 (over x, core), gy: 4 (over z), gz: 2 (over y).
Axes of the slice: x: 2, y: 2, z: 4, core: 2. Of those that a mesh axis runs over, the one named last changes fastest.
Arguments:
- orbitals: float32 [16, 32, 32, 512], P(None, 'gx', 'gy', 'gz'), may hold values from -10 to 10
- potential: float32 [32, 32, 512], P('gx', 'gy', 'gz'), may hold values from 0 to 12
Outputs:
- updated: float32 [16, 32, 32, 512], P(None, 'gx', 'gy', 'gz')
- trial_energies: float32 [16], replicated
All inputs are finite; a program needn't handle non-finite values.
Results may differ from a plain program's by a relative error of at most 0.000022.
Values sent between devices are 32-bit elements; how exact they have to be, the bound alone decides.
A program may use at most 64 MiB of HBM per device.

v0:
```python
import jax
import jax.numpy as jnp
from jax import lax
from jax.sharding import PartitionSpec as P

COARSE_SWEEPS = 4
CENTRE_COEF = -2.5
NEAR_COEF = 4.0 / 3.0
FAR_COEF = -1.0 / 12.0
WEIGHT = 0.8
FINE_DIAG = 4.0
COARSE_DIAG = 1.75
EPSILON = 1e-06


def with_halo(block, sides, width):
    for axis, dim in sides:
        count = lax.axis_size(axis)
        forward = [(i, i + 1) for i in range(count - 1)]
        forward.append((count - 1, 0))
        backward = [(target, source) for source, target in forward]
        low = lax.ppermute(
            lax.slice_in_dim(block, block.shape[dim] - width, None, axis=dim), axis, forward
        )
        high = lax.ppermute(lax.slice_in_dim(block, 0, width, axis=dim), axis, backward)
        block = jnp.concatenate([low, block, high], axis=dim)
    return block


def neighbor(padded, margin, dimension, offset, extent):
    starts = [0, margin, margin, margin]
    starts[dimension] = margin + offset
    limits = [opening + length for opening, length in zip(starts, extent)]
    return lax.slice(padded, starts, limits)


def hamiltonian(values, potential):
    padded = with_halo(values, (("gx", 1), ("gy", 2), ("gz", 3)), 2)
    summed = 3.0 * CENTRE_COEF * values
    for dimension in (1, 2, 3):
        summed = summed + NEAR_COEF * (
            neighbor(padded, 2, dimension, -1, values.shape)
            + neighbor(padded, 2, dimension, 1, values.shape)
        )
        summed = summed + FAR_COEF * (
            neighbor(padded, 2, dimension, -2, values.shape)
            + neighbor(padded, 2, dimension, 2, values.shape)
        )
    return -0.5 * summed + potential[None] * values


def around_cells(padded, extent):
    beside_all = jnp.zeros(extent, jnp.float32)
    for dimension in (1, 2, 3):
        beside_all = (
            beside_all
            + neighbor(padded, 1, dimension, -1, extent)
            + neighbor(padded, 1, dimension, 1, extent)
        )
    return beside_all


def fine_operator(values):
    padded = with_halo(values, (("gx", 1), ("gy", 2), ("gz", 3)), 1)
    return FINE_DIAG * values - 0.5 * around_cells(padded, values.shape)


def coarse_operator(values):
    padded = with_halo(values, (("gx", 1), ("gy", 2), ("gz", 3)), 1)
    return COARSE_DIAG * values - 0.125 * around_cells(padded, values.shape)


def precondition(residual):
    smoothed = WEIGHT * residual / FINE_DIAG
    remainder = residual - fine_operator(smoothed)
    bands, size_x, size_y, size_z = remainder.shape
    blocked = (bands, size_x // 2, 2, size_y // 2, 2, size_z // 2, 2)
    coarse_res = remainder.reshape(blocked).mean(axis=(2, 4, 6))
    approx = WEIGHT * coarse_res / COARSE_DIAG
    for sweep_index in range(COARSE_SWEEPS - 1):
        approx = approx + WEIGHT * (coarse_res - coarse_operator(approx)) / COARSE_DIAG
    lifted = jnp.broadcast_to(approx[:, :, None, :, None, :, None], blocked).reshape(
        remainder.shape
    )
    second = smoothed + lifted
    return second + WEIGHT * (residual - fine_operator(second)) / FINE_DIAG


def inner_product(left, right):
    return jnp.sum(left * right, axis=(1, 2, 3))


def expand(vector):
    return vector[:, None, None, None]


def body(orbitals, potential):
    applied = hamiltonian(orbitals, potential)
    first_sums = lax.psum(
        jnp.stack([inner_product(orbitals, orbitals), inner_product(orbitals, applied)]),
        ("gx", "gy", "gz"),
    )
    norm_orbitals = first_sums[0]
    energy = first_sums[1] / (norm_orbitals + EPSILON)
    residual = applied - expand(energy) * orbitals
    corrected = precondition(residual)
    applied_corr = hamiltonian(corrected, potential)
    response = applied_corr - expand(energy) * corrected
    correlations = lax.psum(
        jnp.stack(
            [
                inner_product(residual, response),
                inner_product(response, response),
                inner_product(orbitals, corrected),
                inner_product(corrected, corrected),
                inner_product(orbitals, applied_corr),
                inner_product(corrected, applied),
                inner_product(corrected, applied_corr),
                inner_product(residual, orbitals),
                inner_product(residual, corrected),
                inner_product(response, orbitals),
                inner_product(response, corrected),
            ]
        ),
        ("gx", "gy", "gz"),
    )
    lambda_step = -correlations[0] / (correlations[1] + EPSILON)
    trial_norm = (
        norm_orbitals
        + 2.0 * lambda_step * correlations[2]
        + lambda_step * lambda_step * correlations[3]
    )
    trial_sum = (
        first_sums[1]
        + lambda_step * (correlations[4] + correlations[5])
        + lambda_step * lambda_step * correlations[6]
    )
    trial_energies = trial_sum / (trial_norm + EPSILON)
    change = trial_energies - energy
    trial_wave = orbitals + expand(lambda_step) * corrected
    residual_change = expand(lambda_step) * response - expand(change) * trial_wave
    projected = lambda_step * correlations[0] - change * (
        correlations[7] + lambda_step * correlations[8]
    )
    cross_term = correlations[9] + lambda_step * correlations[10]
    change_norm = (
        lambda_step * lambda_step * correlations[1]
        - 2.0 * lambda_step * change * cross_term
        + change * change * trial_norm
    )
    mixing_coef = -projected / (change_norm + EPSILON)
    mixed_res = residual + expand(mixing_coef) * residual_change
    updated = (
        orbitals
        + expand(mixing_coef * lambda_step) * corrected
        + expand(lambda_step) * precondition(mixed_res)
    )
    return (updated, trial_energies)


def solution(mesh):
    return jax.shard_map(
        body,
        mesh=mesh,
        in_specs=(P(None, "gx", "gy", "gz"), P("gx", "gy", "gz")),
        out_specs=(P(None, "gx", "gy", "gz"), P()),
        check_vma=False,
    )
```

profile of v0, /device:TPU:0, one launch (start us, length us, event | category | flops | bytes accessed | tf_op | source)
XLA Modules:
  0.0 567.6 jit_solution(9485600245943928243)
XLA Ops:
  15.4 9.3 %collective-permute-done.3 = f32[16,12,2,256]{3,0,2,1:T(8,128)S(1)} collective-permute-done((f32[16,12,2,256]{3,0,2,1:T(8,128)S(1)}, f32[16,12,2,256]{3,0,2,1:T(8,128)S(1)}, u32[]{:S(2)}, u32[]{:S(2)}) %collective-permute-start.3) | collective-permute-done | bytes 393248 | tf_op jit(solution)/shard_map/ppermute | solution.py:25
  25.0 8.7 %collective-permute-done.2 = f32[16,12,2,256]{3,0,2,1:T(8,128)S(1)} collective-permute-done((f32[16,12,2,256]{3,0,2,1:T(8,128)S(1)}, f32[16,12,2,256]{3,0,2,1:T(8,128)S(1)}, u32[]{:S(2)}, u32[]{:S(2)}) %collective-permute-start.2) | collective-permute-done | bytes 393248 | tf_op jit(solution)/shard_map/ppermute | solution.py:22
  53.4 7.4 %multiply_reduce_fusion.12 = (f32[16]{0:T(128)S(1)}, f32[16]{0:T(128)S(1)}, f32[16,8,8,256]{3,2,1,0:T(8,128)}) fusion(f32[16,8,8,256]{3,2,1,0:T(8,128)S(1)} %copy-done, f32[8,8,256]{2,1,0:T(8,128)S(1)} %copy-done.17, f32[16,12,12,2]{3,2,1,0:T(8,128)} %copy.716, f32[16,12,2,256]{3,2,1,0:T(2,128)S(1)} %copy.710, f32[16,12,8,256]{3,2,1,0:T(8,128)S(1)} %get-tuple-element.88, ...), kind=kLoop, calls=%fused_computation.203 | loop fusion | flops 11010016 | bytes 8753280 | tf_op jit(solution)/shard_map/reduce_sum | solution.py:90
  60.8 39.4 %psum.14 = f32[2,16]{1,0:T(2,128)S(1)} all-reduce(f32[2,16]{1,0:T(2,128)S(1)} %pad_maximum_fusion.251), channel_id=1, replica_groups=mesh['gx'=4,'gy'=4,'gz'=2] {'gx','gy','gz'}, use_global_device_ids=true, to_apply=%region_2.0 | all-reduce | flops 32 | bytes 256 | tf_op jit(solution)/shard_map/psum | solution.py:99
  109.9 4.6 collective-permute-done.9
  138.6 6.0 %copy.727 = f32[16,8,8,256]{0,3,2,1:T(8,128)} copy(f32[16,8,8,256]{3,2,1,0:T(8,128)} %fusion.53) | data formatting | bytes 2097152 | tf_op jit(solution)/shard_map/sub | solution.py:75
  144.7 8.7 %reduce_sum.137 = f32[16,4,4,128]{0,3,2,1:T(8,128)S(1)} reduce(f32[16,4,2,4,2,128,2]{0,6,5,4,3,2,1:T(2,128)} %bitcast.133, f32[]{:T(128)} %constant.50.clone.1), dimensions={2,4,6}, to_apply=%region_3.0 | reduce | flops 229376 | bytes 1179652 | tf_op jit(solution)/shard_map/reduce_sum | solution.py:78
  165.9 7.9 %collective-permute-done.16 = f32[16,6,6,1]{3,0,2,1:T(8,128)S(1)} collective-permute-done((f32[16,6,6,1]{3,0,2,1:T(8,128)S(1)}, f32[16,6,6,1]{3,0,2,1:T(8,128)S(1)}, u32[]{:S(2)}, u32[]{:S(2)}) %collective-permute-start.16) | collective-permute-done | bytes 2336 | tf_op jit(solution)/shard_map/ppermute | solution.py:22
  173.7 5.7 %collective-permute-done.17 = f32[16,6,6,1]{3,0,2,1:T(8,128)S(1)} collective-permute-done((f32[16,6,6,1]{3,0,2,1:T(8,128)S(1)}, f32[16,6,6,1]{3,0,2,1:T(8,128)S(1)}, u32[]{:S(2)}, u32[]{:S(2)}) %collective-permute-start.17) | collective-permute-done | bytes 2336 | tf_op jit(solution)/shard_map/ppermute | solution.py:25
  192.3 7.9 %collective-permute-done.22 = f32[16,6,6,1]{3,0,2,1:T(8,128)S(1)} collective-permute-done((f32[16,6,6,1]{3,0,2,1:T(8,128)S(1)}, f32[16,6,6,1]{3,0,2,1:T(8,128)S(1)}, u32[]{:S(2)}, u32[]{:S(2)}) %collective-permute-start.22) | collective-permute-done | bytes 2336 | tf_op jit(solution)/shard_map/ppermute | solution.py:22
  200.2 5.5 collective-permute-done.23
  218.0 7.9 %collective-permute-done.28 = f32[16,6,6,1]{3,0,2,1:T(8,128)S(1)} collective-permute-done((f32[16,6,6,1]{3,0,2,1:T(8,128)S(1)}, f32[16,6,6,1]{3,0,2,1:T(8,128)S(1)}, u32[]{:S(2)}, u32[]{:S(2)}) %collective-permute-start.28) | collective-permute-done | bytes 2336 | tf_op jit(solution)/shard_map/ppermute | solution.py:22
  225.8 5.2 collective-permute-done.29
  231.6 7.5 %broadcast_in_dim.4 = f32[16,4,2,4,2,128,2]{0,6,5,4,3,2,1:T(2,128)} broadcast(f32[16,4,4,128]{0,3,2,1:T(8,128)S(1)} %copy.731), dimensions={0,1,3,5} | broadcast | bytes 1179648 | tf_op jit(solution)/shard_map/broadcast_in_dim | solution.py:82
  239.0 6.1 %copy.732 = f32[16,8,8,256]{3,2,1,0:T(8,128)} copy(f32[16,8,8,256]{0,3,2,1:T(8,128)} %bitcast.134) | data formatting | bytes 2097152 | tf_op jit(solution)/shard_map/reshape | solution.py:82
  277.5 6.5 %fusion.45 = f32[16,8,8,256]{3,2,1,0:T(8,128)S(1)} fusion(f32[16,8,8,256]{3,2,1,0:T(8,128)} %copy-done.1, f32[16,8,8,256]{3,2,1,0:T(8,128)S(1)} %get-tuple-element.32, f32[16,10,10,1]{3,2,1,0:T(8,128)} %copy.742, f32[16,10,1,256]{3,2,1,0:T(1,128)S(1)} %copy.736, f32[16,10,1,256]{3,2,1,0:T(1,128)S(1)} %copy.734, f32[16,1,8,256]{3,2,1,0:T(8,128)} %copy-done.16, ...), kind=kLoop, calls=%fused_computation.112 | loop fusion | flops 7602176 | bytes 3748352 | tf_op jit(solution)/shard_map/add | solution.py:86
  285.8 5.3 collective-permute-done.36
  294.3 9.6 %collective-permute-done.39 = f32[16,12,2,256]{3,0,2,1:T(8,128)S(1)} collective-permute-done((f32[16,12,2,256]{3,0,2,1:T(8,128)S(1)}, f32[16,12,2,256]{3,0,2,1:T(8,128)S(1)}, u32[]{:S(2)}, u32[]{:S(2)}) %collective-permute-start.39) | collective-permute-done | bytes 393248 | tf_op jit(solution)/shard_map/ppermute | solution.py:25
  304.1 8.1 %collective-permute-done.38 = f32[16,12,2,256]{3,0,2,1:T(8,128)S(1)} collective-permute-done((f32[16,12,2,256]{3,0,2,1:T(8,128)S(1)}, f32[16,12,2,256]{3,0,2,1:T(8,128)S(1)}, u32[]{:S(2)}, u32[]{:S(2)}) %collective-permute-start.38) | collective-permute-done | bytes 393248 | tf_op jit(solution)/shard_map/ppermute | solution.py:22
  332.2 8.3 %multiply_reduce_fusion = (f32[16]{0:T(128)S(1)}, f32[16]{0:T(128)S(1)}, f32[16]{0:T(128)}, f32[16]{0:T(128)}, f32[16]{0:T(128)}, /*index=5*/f32[16]{0:T(128)}, ...) fusion(f32[16,8,8,256]{3,2,1,0:T(8,128)S(1)} %fusion.45, ...), kind=kLoop, calls=%fused_computation.189 | loop fusion | flops 21495632 | bytes 6656768 | tf_op jit(solution)/shard_map/reduce_sum | solution.py:90
  341.9 39.6 %psum.15 = f32[11,16]{1,0:T(8,128)S(1)} all-reduce(f32[11,16]{1,0:T(8,128)S(1)} %stack.59), channel_id=1, replica_groups=mesh['gx'=4,'gy'=4,'gz'=2] {'gx','gy','gz'}, use_global_device_ids=true, to_apply=%region_15.0 | all-reduce | flops 176 | bytes 1408 | tf_op jit(solution)/shard_map/psum | solution.py:109
  422.2 6.0 %copy.763 = f32[16,8,8,256]{0,3,2,1:T(8,128)} copy(f32[16,8,8,256]{3,2,1,0:T(8,128)} %fusion.27) | data formatting | bytes 2097152 | tf_op jit(solution)/shard_map/sub | solution.py:75
  428.2 8.7 %reduce_sum.149 = f32[16,4,4,128]{0,3,2,1:T(8,128)S(1)} reduce(f32[16,4,2,4,2,128,2]{0,6,5,4,3,2,1:T(2,128)} %bitcast.132, f32[]{:T(128)} %constant.50.clone.1), dimensions={2,4,6}, to_apply=%region_16.0 | reduce | flops 229376 | bytes 1179652 | tf_op jit(solution)/shard_map/reduce_sum | solution.py:78
  449.8 7.9 %collective-permute-done.52 = f32[16,6,6,1]{3,0,2,1:T(8,128)S(1)} collective-permute-done((f32[16,6,6,1]{3,0,2,1:T(8,128)S(1)}, f32[16,6,6,1]{3,0,2,1:T(8,128)S(1)}, u32[]{:S(2)}, u32[]{:S(2)}) %collective-permute-start.52) | collective-permute-done | bytes 2336 | tf_op jit(solution)/shard_map/ppermute | solution.py:22
  457.7 5.5 collective-permute-done.53
  475.4 7.9 %collective-permute-done.58 = f32[16,6,6,1]{3,0,2,1:T(8,128)S(1)} collective-permute-done((f32[16,6,6,1]{3,0,2,1:T(8,128)S(1)}, f32[16,6,6,1]{3,0,2,1:T(8,128)S(1)}, u32[]{:S(2)}, u32[]{:S(2)}) %collective-permute-start.58) | collective-permute-done | bytes 2336 | tf_op jit(solution)/shard_map/ppermute | solution.py:22
  483.3 5.2 collective-permute-done.59
  501.5 7.9 %collective-permute-done.64 = f32[16,6,6,1]{3,0,2,1:T(8,128)S(1)} collective-permute-done((f32[16,6,6,1]{3,0,2,1:T(8,128)S(1)}, f32[16,6,6,1]{3,0,2,1:T(8,128)S(1)}, u32[]{:S(2)}, u32[]{:S(2)}) %collective-permute-start.64) | collective-permute-done | bytes 2336 | tf_op jit(solution)/shard_map/ppermute | solution.py:22
  509.4 5.2 collective-permute-done.65
  515.1 7.5 %broadcast_in_dim.5 = f32[16,4,2,4,2,128,2]{0,6,5,4,3,2,1:T(2,128)} broadcast(f32[16,4,4,128]{0,3,2,1:T(8,128)S(1)} %copy.767), dimensions={0,1,3,5} | broadcast | bytes 1179648 | tf_op jit(solution)/shard_map/broadcast_in_dim | solution.py:82
  522.5 6.1 %copy.768 = f32[16,8,8,256]{3,2,1,0:T(8,128)} copy(f32[16,8,8,256]{0,3,2,1:T(8,128)} %bitcast.135) | data formatting | bytes 2097152 | tf_op jit(solution)/shard_map/reshape | solution.py:82
  539.0 4.6 collective-permute-done.69
  (283 shorter events, 278.5 us)
Async XLA Ops:
  1.8 6.7 %collective-permute-start = (f32[16,2,8,256]{3,2,1,0:T(8,128)S(1)}, f32[16,2,8,256]{3,2,1,0:T(8,128)S(1)}, u32[]{:S(2)}, u32[]{:S(2)}) collective-permute-start(f32[16,2,8,256]{3,2,1,0:T(8,128)S(1)} %get-tuple-element.72), channel_id=1, source_target_pairs={{0,8},{8,16},{16,24},{24,0},{1,9},{9,17},{17,25},{25,1},{2,10},{10... | collective-permute-start | bytes 786440 | tf_op jit(solution)/shard_map/ppermute | solution.py:22
  2.3 8.6 %collective-permute-start.1 = (f32[16,2,8,256]{3,2,1,0:T(8,128)S(1)}, f32[16,2,8,256]{3,2,1,0:T(8,128)S(1)}, u32[]{:S(2)}, u32[]{:S(2)}) collective-permute-start(f32[16,2,8,256]{3,2,1,0:T(8,128)S(1)} %get-tuple-element.71), channel_id=1, source_target_pairs={{8,0},{16,8},{24,16},{0,24},{9,1},{17,9},{25,17},{1,25},{10,2},{18... | collective-permute-start | bytes 786440 | tf_op jit(solution)/shard_map/ppermute | solution.py:25
  11.4 13.3 %collective-permute-start.3 = (f32[16,12,2,256]{3,0,2,1:T(8,128)S(1)}, f32[16,12,2,256]{3,0,2,1:T(8,128)S(1)}, u32[]{:S(2)}, u32[]{:S(2)}) collective-permute-start(f32[16,12,2,256]{3,0,2,1:T(8,128)S(1)} %copy.780), channel_id=1, source_target_pairs={{2,0},{4,2},{6,4},{0,6},{3,1},{5,3},{7,5},{1,7},{10,8},{12,10},{14... | collective-permute-start | bytes 1179656 | tf_op jit(solution)/shard_map/ppermute | solution.py:25
  15.3 18.4 %collective-permute-start.2 = (f32[16,12,2,256]{3,0,2,1:T(8,128)S(1)}, f32[16,12,2,256]{3,0,2,1:T(8,128)S(1)}, u32[]{:S(2)}, u32[]{:S(2)}) collective-permute-start(f32[16,12,2,256]{3,0,2,1:T(8,128)S(1)} %copy.779), channel_id=1, source_target_pairs={{0,2},{2,4},{4,6},{6,0},{1,3},{3,5},{5,7},{7,1},{8,10},{10,12},{12... | collective-permute-start | bytes 1179656 | tf_op jit(solution)/shard_map/ppermute | solution.py:22
  107.6 6.9 %collective-permute-start.9 = (f32[16,10,1,256]{3,0,2,1:T(8,128)S(1)}, f32[16,10,1,256]{3,0,2,1:T(8,128)S(1)}, u32[]{:S(2)}, u32[]{:S(2)}) collective-permute-start(f32[16,10,1,256]{3,0,2,1:T(8,128)S(1)} %copy.719), channel_id=1, source_target_pairs={{2,0},{4,2},{6,4},{0,6},{3,1},{5,3},{7,5},{1,7},{10,8},{12,10},{14... | collective-permute-start | bytes 491528 | tf_op jit(solution)/shard_map/ppermute | solution.py:25
  109.2 9.4 %collective-permute-start.8 = (f32[16,10,1,256]{3,0,2,1:T(8,128)S(1)}, f32[16,10,1,256]{3,0,2,1:T(8,128)S(1)}, u32[]{:S(2)}, u32[]{:S(2)}) collective-permute-start(f32[16,10,1,256]{3,0,2,1:T(8,128)S(1)} %copy.717), channel_id=1, source_target_pairs={{0,2},{2,4},{4,6},{6,0},{1,3},{3,5},{5,7},{7,1},{8,10},{10,12},{12... | collective-permute-start | bytes 491528 | tf_op jit(solution)/shard_map/ppermute | solution.py:22
  163.8 9.9 %collective-permute-start.16 = (f32[16,6,6,1]{3,0,2,1:T(8,128)S(1)}, f32[16,6,6,1]{3,0,2,1:T(8,128)S(1)}, u32[]{:S(2)}, u32[]{:S(2)}) collective-permute-start(f32[16,6,6,1]{3,0,2,1:T(8,128)S(1)} %get-tuple-element.83), channel_id=1, source_target_pairs={{0,1},{1,0},{2,3},{3,2},{4,5},{5,4},{6,7},{7,6},{8,9},{9,8},{10,11... | collective-permute-start | bytes 6920 | tf_op jit(solution)/shard_map/ppermute | solution.py:22
  164.2 15.3 %collective-permute-start.17 = (f32[16,6,6,1]{3,0,2,1:T(8,128)S(1)}, f32[16,6,6,1]{3,0,2,1:T(8,128)S(1)}, u32[]{:S(2)}, u32[]{:S(2)}) collective-permute-start(f32[16,6,6,1]{3,0,2,1:T(8,128)S(1)} %get-tuple-element.84), channel_id=1, source_target_pairs={{1,0},{0,1},{3,2},{2,3},{5,4},{4,5},{7,6},{6,7},{9,8},{8,9},{11,10... | collective-permute-start | bytes 6920 | tf_op jit(solution)/shard_map/ppermute | solution.py:25
  190.2 9.9 %collective-permute-start.22 = (f32[16,6,6,1]{3,0,2,1:T(8,128)S(1)}, f32[16,6,6,1]{3,0,2,1:T(8,128)S(1)}, u32[]{:S(2)}, u32[]{:S(2)}) collective-permute-start(f32[16,6,6,1]{3,0,2,1:T(8,128)S(1)} %get-tuple-element.81), channel_id=1, source_target_pairs={{0,1},{1,0},{2,3},{3,2},{4,5},{5,4},{6,7},{7,6},{8,9},{9,8},{10,11... | collective-permute-start | bytes 6920 | tf_op jit(solution)/shard_map/ppermute | solution.py:22
  191.1 14.6 %collective-permute-start.23 = (f32[16,6,6,1]{3,0,2,1:T(8,128)S(1)}, f32[16,6,6,1]{3,0,2,1:T(8,128)S(1)}, u32[]{:S(2)}, u32[]{:S(2)}) collective-permute-start(f32[16,6,6,1]{3,0,2,1:T(8,128)S(1)} %get-tuple-element.82), channel_id=1, source_target_pairs={{1,0},{0,1},{3,2},{2,3},{5,4},{4,5},{7,6},{6,7},{9,8},{8,9},{11,10... | collective-permute-start | bytes 6920 | tf_op jit(solution)/shard_map/ppermute | solution.py:25
  209.2 6.5 %collective-permute-start.26 = (f32[16,6,1,128]{3,0,2,1:T(8,128)S(1)}, f32[16,6,1,128]{3,0,2,1:T(8,128)S(1)}, u32[]{:S(2)}, u32[]{:S(2)}) collective-permute-start(f32[16,6,1,128]{3,0,2,1:T(8,128)S(1)} %get-tuple-element.95), channel_id=1, source_target_pairs={{0,2},{2,4},{4,6},{6,0},{1,3},{3,5},{5,7},{7,1},{8,10},{10,12},{12... | collective-permute-start | bytes 147464 | tf_op jit(solution)/shard_map/ppermute | solution.py:22
  215.9 9.9 %collective-permute-start.28 = (f32[16,6,6,1]{3,0,2,1:T(8,128)S(1)}, f32[16,6,6,1]{3,0,2,1:T(8,128)S(1)}, u32[]{:S(2)}, u32[]{:S(2)}) collective-permute-start(f32[16,6,6,1]{3,0,2,1:T(8,128)S(1)} %get-tuple-element.79), channel_id=1, source_target_pairs={{0,1},{1,0},{2,3},{3,2},{4,5},{5,4},{6,7},{7,6},{8,9},{9,8},{10,11... | collective-permute-start | bytes 6920 | tf_op jit(solution)/shard_map/ppermute | solution.py:22
  216.7 14.3 %collective-permute-start.29 = (f32[16,6,6,1]{3,0,2,1:T(8,128)S(1)}, f32[16,6,6,1]{3,0,2,1:T(8,128)S(1)}, u32[]{:S(2)}, u32[]{:S(2)}) collective-permute-start(f32[16,6,6,1]{3,0,2,1:T(8,128)S(1)} %get-tuple-element.80), channel_id=1, source_target_pairs={{1,0},{0,1},{3,2},{2,3},{5,4},{4,5},{7,6},{6,7},{9,8},{8,9},{11,10... | collective-permute-start | bytes 6920 | tf_op jit(solution)/shard_map/ppermute | solution.py:25
  251.5 7.7 %collective-permute-start.33 = (f32[16,10,1,256]{3,0,2,1:T(8,128)S(1)}, f32[16,10,1,256]{3,0,2,1:T(8,128)S(1)}, u32[]{:S(2)}, u32[]{:S(2)}) collective-permute-start(f32[16,10,1,256]{3,0,2,1:T(8,128)S(1)} %copy.735), channel_id=1, source_target_pairs={{2,0},{4,2},{6,4},{0,6},{3,1},{5,3},{7,5},{1,7},{10,8},{12,10},{14... | collective-permute-start | bytes 491528 | tf_op jit(solution)/shard_map/ppermute | solution.py:25
  254.8 8.9 %collective-permute-start.32 = (f32[16,10,1,256]{3,0,2,1:T(8,128)S(1)}, f32[16,10,1,256]{3,0,2,1:T(8,128)S(1)}, u32[]{:S(2)}, u32[]{:S(2)}) collective-permute-start(f32[16,10,1,256]{3,0,2,1:T(8,128)S(1)} %copy.733), channel_id=1, source_target_pairs={{0,2},{2,4},{4,6},{6,0},{1,3},{3,5},{5,7},{7,1},{8,10},{10,12},{12... | collective-permute-start | bytes 491528 | tf_op jit(solution)/shard_map/ppermute | solution.py:22
  284.0 7.1 %collective-permute-start.36 = (f32[16,2,8,256]{3,2,1,0:T(8,128)S(1)}, f32[16,2,8,256]{3,2,1,0:T(8,128)S(1)}, u32[]{:S(2)}, u32[]{:S(2)}) collective-permute-start(f32[16,2,8,256]{3,2,1,0:T(8,128)S(1)} %get-tuple-element.62), channel_id=1, source_target_pairs={{0,8},{8,16},{16,24},{24,0},{1,9},{9,17},{17,25},{25,1},{2,10},{10... | collective-permute-start | bytes 786440 | tf_op jit(solution)/shard_map/ppermute | solution.py:22
  284.1 7.3 %collective-permute-start.37 = (f32[16,2,8,256]{3,2,1,0:T(8,128)S(1)}, f32[16,2,8,256]{3,2,1,0:T(8,128)S(1)}, u32[]{:S(2)}, u32[]{:S(2)}) collective-permute-start(f32[16,2,8,256]{3,2,1,0:T(8,128)S(1)} %get-tuple-element.63), channel_id=1, source_target_pairs={{8,0},{16,8},{24,16},{0,24},{9,1},{17,9},{25,17},{1,25},{10,2},{18... | collective-permute-start | bytes 786440 | tf_op jit(solution)/shard_map/ppermute | solution.py:25
  291.8 12.0 %collective-permute-start.39 = (f32[16,12,2,256]{3,0,2,1:T(8,128)S(1)}, f32[16,12,2,256]{3,0,2,1:T(8,128)S(1)}, u32[]{:S(2)}, u32[]{:S(2)}) collective-permute-start(f32[16,12,2,256]{3,0,2,1:T(8,128)S(1)} %copy.745), channel_id=1, source_target_pairs={{2,0},{4,2},{6,4},{0,6},{3,1},{5,3},{7,5},{1,7},{10,8},{12,10},{14... | collective-permute-start | bytes 1179656 | tf_op jit(solution)/shard_map/ppermute | solution.py:25
  293.9 18.3 %collective-permute-start.38 = (f32[16,12,2,256]{3,0,2,1:T(8,128)S(1)}, f32[16,12,2,256]{3,0,2,1:T(8,128)S(1)}, u32[]{:S(2)}, u32[]{:S(2)}) collective-permute-start(f32[16,12,2,256]{3,0,2,1:T(8,128)S(1)} %copy.743), channel_id=1, source_target_pairs={{0,2},{2,4},{4,6},{6,0},{1,3},{3,5},{5,7},{7,1},{8,10},{10,12},{12... | collective-permute-start | bytes 1179656 | tf_op jit(solution)/shard_map/ppermute | solution.py:22
  318.5 6.4 %collective-permute-start.40 = (f32[16,12,12,2]{0,3,2,1:T(2,128)}, f32[16,12,12,2]{0,3,2,1:T(2,128)}, u32[]{:S(2)}, u32[]{:S(2)}) collective-permute-start(f32[16,12,12,2]{0,3,2,1:T(2,128)} %copy.749), channel_id=1, source_target_pairs={{0,1},{1,0},{2,3},{3,2},{4,5},{5,4},{6,7},{7,6},{8,9},{9,8},{10,11... | collective-permute-start | bytes 55304 | tf_op jit(solution)/shard_map/ppermute | solution.py:22
  390.5 6.9 %collective-permute-start.45 = (f32[16,10,1,256]{3,0,2,1:T(8,128)S(1)}, f32[16,10,1,256]{3,0,2,1:T(8,128)S(1)}, u32[]{:S(2)}, u32[]{:S(2)}) collective-permute-start(f32[16,10,1,256]{3,0,2,1:T(8,128)S(1)} %copy.755), channel_id=1, source_target_pairs={{2,0},{4,2},{6,4},{0,6},{3,1},{5,3},{7,5},{1,7},{10,8},{12,10},{14... | collective-permute-start | bytes 491528 | tf_op jit(solution)/shard_map/ppermute | solution.py:25
  392.9 9.1 %collective-permute-start.44 = (f32[16,10,1,256]{3,0,2,1:T(8,128)S(1)}, f32[16,10,1,256]{3,0,2,1:T(8,128)S(1)}, u32[]{:S(2)}, u32[]{:S(2)}) collective-permute-start(f32[16,10,1,256]{3,0,2,1:T(8,128)S(1)} %copy.753), channel_id=1, source_target_pairs={{0,2},{2,4},{4,6},{6,0},{1,3},{3,5},{5,7},{7,1},{8,10},{10,12},{12... | collective-permute-start | bytes 491528 | tf_op jit(solution)/shard_map/ppermute | solution.py:22
  447.7 9.9 %collective-permute-start.52 = (f32[16,6,6,1]{3,0,2,1:T(8,128)S(1)}, f32[16,6,6,1]{3,0,2,1:T(8,128)S(1)}, u32[]{:S(2)}, u32[]{:S(2)}) collective-permute-start(f32[16,6,6,1]{3,0,2,1:T(8,128)S(1)} %get-tuple-element.77), channel_id=1, source_target_pairs={{0,1},{1,0},{2,3},{3,2},{4,5},{5,4},{6,7},{7,6},{8,9},{9,8},{10,11... | collective-permute-start | bytes 6920 | tf_op jit(solution)/shard_map/ppermute | solution.py:22
  448.2 15.0 %collective-permute-start.53 = (f32[16,6,6,1]{3,0,2,1:T(8,128)S(1)}, f32[16,6,6,1]{3,0,2,1:T(8,128)S(1)}, u32[]{:S(2)}, u32[]{:S(2)}) collective-permute-start(f32[16,6,6,1]{3,0,2,1:T(8,128)S(1)} %get-tuple-element.78), channel_id=1, source_target_pairs={{1,0},{0,1},{3,2},{2,3},{5,4},{4,5},{7,6},{6,7},{9,8},{8,9},{11,10... | collective-permute-start | bytes 6920 | tf_op jit(solution)/shard_map/ppermute | solution.py:25
  466.8 6.4 %collective-permute-start.56 = (f32[16,6,1,128]{3,0,2,1:T(8,128)S(1)}, f32[16,6,1,128]{3,0,2,1:T(8,128)S(1)}, u32[]{:S(2)}, u32[]{:S(2)}) collective-permute-start(f32[16,6,1,128]{3,0,2,1:T(8,128)S(1)} %get-tuple-element.91), channel_id=1, source_target_pairs={{0,2},{2,4},{4,6},{6,0},{1,3},{3,5},{5,7},{7,1},{8,10},{10,12},{12... | collective-permute-start | bytes 147464 | tf_op jit(solution)/shard_map/ppermute | solution.py:22
  473.4 9.9 %collective-permute-start.58 = (f32[16,6,6,1]{3,0,2,1:T(8,128)S(1)}, f32[16,6,6,1]{3,0,2,1:T(8,128)S(1)}, u32[]{:S(2)}, u32[]{:S(2)}) collective-permute-start(f32[16,6,6,1]{3,0,2,1:T(8,128)S(1)} %get-tuple-element.75), channel_id=1, source_target_pairs={{0,1},{1,0},{2,3},{3,2},{4,5},{5,4},{6,7},{7,6},{8,9},{9,8},{10,11... | collective-permute-start | bytes 6920 | tf_op jit(solution)/shard_map/ppermute | solution.py:22
  473.9 14.6 %collective-permute-start.59 = (f32[16,6,6,1]{3,0,2,1:T(8,128)S(1)}, f32[16,6,6,1]{3,0,2,1:T(8,128)S(1)}, u32[]{:S(2)}, u32[]{:S(2)}) collective-permute-start(f32[16,6,6,1]{3,0,2,1:T(8,128)S(1)} %get-tuple-element.76), channel_id=1, source_target_pairs={{1,0},{0,1},{3,2},{2,3},{5,4},{4,5},{7,6},{6,7},{9,8},{8,9},{11,10... | collective-permute-start | bytes 6920 | tf_op jit(solution)/shard_map/ppermute | solution.py:25
  492.1 6.2 %collective-permute-start.62 = (f32[16,6,1,128]{3,0,2,1:T(8,128)S(1)}, f32[16,6,1,128]{3,0,2,1:T(8,128)S(1)}, u32[]{:S(2)}, u32[]{:S(2)}) collective-permute-start(f32[16,6,1,128]{3,0,2,1:T(8,128)S(1)} %get-tuple-element.89), channel_id=1, source_target_pairs={{0,2},{2,4},{4,6},{6,0},{1,3},{3,5},{5,7},{7,1},{8,10},{10,12},{12... | collective-permute-start | bytes 147464 | tf_op jit(solution)/shard_map/ppermute | solution.py:22
  499.4 9.9 %collective-permute-start.64 = (f32[16,6,6,1]{3,0,2,1:T(8,128)S(1)}, f32[16,6,6,1]{3,0,2,1:T(8,128)S(1)}, u32[]{:S(2)}, u32[]{:S(2)}) collective-permute-start(f32[16,6,6,1]{3,0,2,1:T(8,128)S(1)} %get-tuple-element.73), channel_id=1, source_target_pairs={{0,1},{1,0},{2,3},{3,2},{4,5},{5,4},{6,7},{7,6},{8,9},{9,8},{10,11... | collective-permute-start | bytes 6920 | tf_op jit(solution)/shard_map/ppermute | solution.py:22
  499.8 14.7 %collective-permute-start.65 = (f32[16,6,6,1]{3,0,2,1:T(8,128)S(1)}, f32[16,6,6,1]{3,0,2,1:T(8,128)S(1)}, u32[]{:S(2)}, u32[]{:S(2)}) collective-permute-start(f32[16,6,6,1]{3,0,2,1:T(8,128)S(1)} %get-tuple-element.74), channel_id=1, source_target_pairs={{1,0},{0,1},{3,2},{2,3},{5,4},{4,5},{7,6},{6,7},{9,8},{8,9},{11,10... | collective-permute-start | bytes 6920 | tf_op jit(solution)/shard_map/ppermute | solution.py:25
  535.3 8.2 %collective-permute-start.69 = (f32[16,10,1,256]{3,0,2,1:T(8,128)S(1)}, f32[16,10,1,256]{3,0,2,1:T(8,128)S(1)}, u32[]{:S(2)}, u32[]{:S(2)}) collective-permute-start(f32[16,10,1,256]{3,0,2,1:T(8,128)S(1)} %copy.771), channel_id=1, source_target_pairs={{2,0},{4,2},{6,4},{0,6},{3,1},{5,3},{7,5},{1,7},{10,8},{12,10},{14... | collective-permute-start | bytes 491528 | tf_op jit(solution)/shard_map/ppermute | solution.py:25
  538.9 8.6 %collective-permute-start.68 = (f32[16,10,1,256]{3,0,2,1:T(8,128)S(1)}, f32[16,10,1,256]{3,0,2,1:T(8,128)S(1)}, u32[]{:S(2)}, u32[]{:S(2)}) collective-permute-start(f32[16,10,1,256]{3,0,2,1:T(8,128)S(1)} %copy.769), channel_id=1, source_target_pairs={{0,2},{2,4},{4,6},{6,0},{1,3},{3,5},{5,7},{7,1},{8,10},{10,12},{12... | collective-permute-start | bytes 491528 | tf_op jit(solution)/shard_map/ppermute | solution.py:22
  (58 other events, 394.5 us)
where the time goes:
time: 576 us; the launch traced here: 568 us
  waiting for transfers between devices  207 us (36%)
  local copies, waits for them, and re-layouts  125 us (22%)
  starting transfers between devices  89 us (15%)
  blocking collectives  79 us (14%)
  other arithmetic  65.7 us (11%)
    ppermute x36, waiting for transfers between devices, with_halo(): lax.ppermute(lax.slice_in_dim(block, block.shape[dim] - width, None, axis...  126 us
    ppermute x36, waiting for transfers between devices, with_halo(): lax.ppermute(lax.slice_in_dim(block, 0, width, axis=dim), axis, backward)  80.3 us
    ppermute x36, starting transfers between devices, with_halo(): lax.ppermute(lax.slice_in_dim(block, 0, width, axis=dim), axis, backward)  69.4 us
    psum x1, blocking collectives, body(): lax.psum(jnp.stack([inner_product(residual, response), inner_product(resp...  39.6 us
    psum x1, blocking collectives, body(): lax.psum(jnp.stack([inner_product(orbitals, orbitals), inner_product(orbi...  39.4 us
    slice x35, local copies, waits for them, and re-layouts, with_halo(): lax.slice_in_dim(block, block.shape[dim] - width, None, axis=dim)  27.5 us
    ppermute x36, starting transfers between devices, with_halo(): lax.ppermute(lax.slice_in_dim(block, block.shape[dim] - width, None, axis...  19.7 us
    ppermute x12, local copies, waits for them, and re-layouts, with_halo(): lax.ppermute(lax.slice_in_dim(block, 0, width, axis=dim), axis, backward)  19.1 us
  transfers between devices with their start and end apart: 72, of which 59 were waited for; matrix products, arithmetic and copies ran while one was open for 6% of the time, Pallas kernels for 0%

commit v1 on v0

--- a/solution.py
+++ b/solution.py
@@ -11,6 +11,7 @@
 FINE_DIAG = 4.0
 COARSE_DIAG = 1.75
 EPSILON = 1e-06
+shape_bars = lambda array_here, mesh_dim: jnp.sum(lax.all_gather(array_here, mesh_dim), axis=0)
 
 
 def with_halo(block, sides, width):
@@ -96,7 +97,7 @@
 
 def body(orbitals, potential):
     applied = hamiltonian(orbitals, potential)
-    first_sums = lax.psum(
+    first_sums = shape_bars(
         jnp.stack([inner_product(orbitals, orbitals), inner_product(orbitals, applied)]),
         ("gx", "gy", "gz"),
     )

time: 576 us -> 599 us (1.040)
  blocking collectives: 79 us -> 104 us
    all_gather x0 -> x1, blocking collectives: none -> 64.1 us  [lax.all_gather(array_here, mesh_dim)]
    psum x1 -> x0, blocking collectives: 39.4 us -> none  [body(): lax.psum(jnp.stack([inner_product(orbitals, orbitals), inner_product(orbi...]
  transfers between devices with their start and end apart: 72 -> 72, of which waited for: 59 -> 57; matrix products, arithmetic and copies ran while one was open for 6% -> 6% of each run, Pallas kernels for 0% -> 0%
where the time goes in v1:
time: 599 us; the launch traced here: 591 us
  waiting for transfers between devices  205 us (34%)
  local copies, waits for them, and re-layouts  125 us (21%)
  blocking collectives  104 us (17%)
  starting transfers between devices  88.8 us (15%)
  other arithmetic  65.8 us (11%)
    ppermute x36, waiting for transfers between devices, with_halo(): lax.ppermute(lax.slice_in_dim(block, block.shape[dim] - width, None, axis...  123 us
    ppermute x36, waiting for transfers between devices, with_halo(): lax.ppermute(lax.slice_in_dim(block, 0, width, axis=dim), axis, backward)  82.8 us
    ppermute x36, starting transfers between devices, with_halo(): lax.ppermute(lax.slice_in_dim(block, 0, width, axis=dim), axis, backward)  66.2 us
    all_gather x1, blocking collectives, lax.all_gather(array_here, mesh_dim)  64.1 us
    psum x1, blocking collectives, body(): lax.psum(jnp.stack([inner_product(residual, response), inner_product(resp...  39.5 us
    slice x35, local copies, waits for them, and re-layouts, with_halo(): lax.slice_in_dim(block, block.shape[dim] - width, None, axis=dim)  27.5 us
    ppermute x36, starting transfers between devices, with_halo(): lax.ppermute(lax.slice_in_dim(block, block.shape[dim] - width, None, axis...  22.7 us
    ppermute x12, local copies, waits for them, and re-layouts, with_halo(): lax.ppermute(lax.slice_in_dim(block, 0, width, axis=dim), axis, backward)  19.1 us
  transfers between devices with their start and end apart: 72, of which 57 were waited for; matrix products, arithmetic and copies ran while one was open for 6% of the time, Pallas kernels for 0%

profile of v1, /device:TPU:0, one launch (start us, length us, event | category | flops | bytes accessed | tf_op | source)
XLA Modules:
  0.0 590.9 jit_solution(4858735988484426181)
XLA Ops:
  15.4 9.3 %collective-permute-done.3 = f32[16,12,2,256]{3,0,2,1:T(8,128)S(1)} collective-permute-done((f32[16,12,2,256]{3,0,2,1:T(8,128)S(1)}, f32[16,12,2,256]{3,0,2,1:T(8,128)S(1)}, u32[]{:S(2)}, u32[]{:S(2)}) %collective-permute-start.3) | collective-permute-done | bytes 393248 | tf_op jit(solution)/shard_map/ppermute | solution.py:26
  25.0 8.7 %collective-permute-done.2 = f32[16,12,2,256]{3,0,2,1:T(8,128)S(1)} collective-permute-done((f32[16,12,2,256]{3,0,2,1:T(8,128)S(1)}, f32[16,12,2,256]{3,0,2,1:T(8,128)S(1)}, u32[]{:S(2)}, u32[]{:S(2)}) %collective-permute-start.2) | collective-permute-done | bytes 393248 | tf_op jit(solution)/shard_map/ppermute | solution.py:23
  53.4 7.4 %multiply_reduce_fusion.12 = (f32[16]{0:T(128)S(1)}, f32[16]{0:T(128)S(1)}, f32[16,8,8,256]{3,2,1,0:T(8,128)}) fusion(f32[16,8,8,256]{3,2,1,0:T(8,128)S(1)} %copy-done, f32[8,8,256]{2,1,0:T(8,128)S(1)} %copy-done.17, f32[16,12,12,2]{3,2,1,0:T(8,128)} %copy.716, f32[16,12,2,256]{3,2,1,0:T(2,128)S(1)} %copy.710, f32[16,12,8,256]{3,2,1,0:T(8,128)S(1)} %get-tuple-element.88, ...), kind=kLoop, calls=%fused_computation.203 | loop fusion | flops 11010016 | bytes 8753280 | tf_op jit(solution)/shard_map/reduce_sum | solution.py:91
  60.8 64.1 %all-gather.1 = f32[32,2,16]{2,1,0:T(2,128)S(1)} all-gather(f32[1,2,16]{2,1,0:T(2,128)S(1)} %maximum_bitcast_fusion), channel_id=2, replica_groups=mesh['gx'=4,'gy'=4,'gz'=2] {'gx','gy','gz'}, dimensions={0}, use_global_device_ids=true | all-gather | bytes 4224 | tf_op jit(solution)/shard_map/all_gather | solution.py:14
  134.1 8.1 %collective-permute-done.9 = f32[16,10,1,256]{3,0,2,1:T(8,128)S(1)} collective-permute-done((f32[16,10,1,256]{3,0,2,1:T(8,128)S(1)}, f32[16,10,1,256]{3,0,2,1:T(8,128)S(1)}, u32[]{:S(2)}, u32[]{:S(2)}) %collective-permute-start.9) | collective-permute-done | bytes 163872 | tf_op jit(solution)/shard_map/ppermute | solution.py:26
  162.4 6.0 %copy.727 = f32[16,8,8,256]{0,3,2,1:T(8,128)} copy(f32[16,8,8,256]{3,2,1,0:T(8,128)} %fusion.53) | data formatting | bytes 2097152 | tf_op jit(solution)/shard_map/sub | solution.py:76
  168.4 8.7 %reduce_sum.147 = f32[16,4,4,128]{0,3,2,1:T(8,128)S(1)} reduce(f32[16,4,2,4,2,128,2]{0,6,5,4,3,2,1:T(2,128)} %bitcast.135, f32[]{:T(128)} %constant.50.clone.1), dimensions={2,4,6}, to_apply=%region_3.0 | reduce | flops 229376 | bytes 1179652 | tf_op jit(solution)/shard_map/reduce_sum | solution.py:79
  189.2 7.9 %collective-permute-done.16 = f32[16,6,6,1]{3,0,2,1:T(8,128)S(1)} collective-permute-done((f32[16,6,6,1]{3,0,2,1:T(8,128)S(1)}, f32[16,6,6,1]{3,0,2,1:T(8,128)S(1)}, u32[]{:S(2)}, u32[]{:S(2)}) %collective-permute-start.16) | collective-permute-done | bytes 2336 | tf_op jit(solution)/shard_map/ppermute | solution.py:23
  197.0 6.1 %collective-permute-done.17 = f32[16,6,6,1]{3,0,2,1:T(8,128)S(1)} collective-permute-done((f32[16,6,6,1]{3,0,2,1:T(8,128)S(1)}, f32[16,6,6,1]{3,0,2,1:T(8,128)S(1)}, u32[]{:S(2)}, u32[]{:S(2)}) %collective-permute-start.17) | collective-permute-done | bytes 2336 | tf_op jit(solution)/shard_map/ppermute | solution.py:26
  215.3 7.9 %collective-permute-done.22 = f32[16,6,6,1]{3,0,2,1:T(8,128)S(1)} collective-permute-done((f32[16,6,6,1]{3,0,2,1:T(8,128)S(1)}, f32[16,6,6,1]{3,0,2,1:T(8,128)S(1)}, u32[]{:S(2)}, u32[]{:S(2)}) %collective-permute-start.22) | collective-permute-done | bytes 2336 | tf_op jit(solution)/shard_map/ppermute | solution.py:23
  223.1 5.1 collective-permute-done.23
  241.2 7.9 %collective-permute-done.28 = f32[16,6,6,1]{3,0,2,1:T(8,128)S(1)} collective-permute-done((f32[16,6,6,1]{3,0,2,1:T(8,128)S(1)}, f32[16,6,6,1]{3,0,2,1:T(8,128)S(1)}, u32[]{:S(2)}, u32[]{:S(2)}) %collective-permute-start.28) | collective-permute-done | bytes 2336 | tf_op jit(solution)/shard_map/ppermute | solution.py:23
  249.0 5.0 collective-permute-done.29
  254.5 7.5 %broadcast_in_dim.4 = f32[16,4,2,4,2,128,2]{0,6,5,4,3,2,1:T(2,128)} broadcast(f32[16,4,4,128]{0,3,2,1:T(8,128)S(1)} %copy.731), dimensions={0,1,3,5} | broadcast | bytes 1179648 | tf_op jit(solution)/shard_map/broadcast_in_dim | solution.py:83
  262.0 6.1 %copy.732 = f32[16,8,8,256]{3,2,1,0:T(8,128)} copy(f32[16,8,8,256]{0,3,2,1:T(8,128)} %bitcast.136) | data formatting | bytes 2097152 | tf_op jit(solution)/shard_map/reshape | solution.py:83
  278.2 4.6 collective-permute-done.33
  300.4 6.5 %fusion.45 = f32[16,8,8,256]{3,2,1,0:T(8,128)S(1)} fusion(f32[16,8,8,256]{3,2,1,0:T(8,128)} %copy-done.1, f32[16,8,8,256]{3,2,1,0:T(8,128)S(1)} %get-tuple-element.32, f32[16,10,10,1]{3,2,1,0:T(8,128)} %copy.742, f32[16,10,1,256]{3,2,1,0:T(1,128)S(1)} %copy.736, f32[16,10,1,256]{3,2,1,0:T(1,128)S(1)} %copy.734, f32[16,1,8,256]{3,2,1,0:T(8,128)} %copy-done.16, ...), kind=kLoop, calls=%fused_computation.112 | loop fusion | flops 7602176 | bytes 3748352 | tf_op jit(solution)/shard_map/add | solution.py:87
  308.8 5.6 collective-permute-done.36
  317.7 9.5 %collective-permute-done.39 = f32[16,12,2,256]{3,0,2,1:T(8,128)S(1)} collective-permute-done((f32[16,12,2,256]{3,0,2,1:T(8,128)S(1)}, f32[16,12,2,256]{3,0,2,1:T(8,128)S(1)}, u32[]{:S(2)}, u32[]{:S(2)}) %collective-permute-start.39) | collective-permute-done | bytes 393248 | tf_op jit(solution)/shard_map/ppermute | solution.py:26
  327.5 8.2 %collective-permute-done.38 = f32[16,12,2,256]{3,0,2,1:T(8,128)S(1)} collective-permute-done((f32[16,12,2,256]{3,0,2,1:T(8,128)S(1)}, f32[16,12,2,256]{3,0,2,1:T(8,128)S(1)}, u32[]{:S(2)}, u32[]{:S(2)}) %collective-permute-start.38) | collective-permute-done | bytes 393248 | tf_op jit(solution)/shard_map/ppermute | solution.py:23
  355.3 8.3 %multiply_reduce_fusion = (f32[16]{0:T(128)S(1)}, f32[16]{0:T(128)S(1)}, f32[16]{0:T(128)}, f32[16]{0:T(128)}, f32[16]{0:T(128)}, /*index=5*/f32[16]{0:T(128)}, ...) fusion(f32[16,8,8,256]{3,2,1,0:T(8,128)S(1)} %fusion.45, ...), kind=kLoop, calls=%fused_computation.189 | loop fusion | flops 21495632 | bytes 6656768 | tf_op jit(solution)/shard_map/reduce_sum | solution.py:91
  365.0 39.5 %psum.7 = f32[11,16]{1,0:T(8,128)S(1)} all-reduce(f32[11,16]{1,0:T(8,128)S(1)} %stack.59), channel_id=1, replica_groups=mesh['gx'=4,'gy'=4,'gz'=2] {'gx','gy','gz'}, use_global_device_ids=true, to_apply=%region_15.0 | all-reduce | flops 176 | bytes 1408 | tf_op jit(solution)/shard_map/psum | solution.py:110
  445.4 6.0 %copy.763 = f32[16,8,8,256]{0,3,2,1:T(8,128)} copy(f32[16,8,8,256]{3,2,1,0:T(8,128)} %fusion.27) | data formatting | bytes 2097152 | tf_op jit(solution)/shard_map/sub | solution.py:76
  451.4 8.7 %reduce_sum.159 = f32[16,4,4,128]{0,3,2,1:T(8,128)S(1)} reduce(f32[16,4,2,4,2,128,2]{0,6,5,4,3,2,1:T(2,128)} %bitcast.134, f32[]{:T(128)} %constant.50.clone.1), dimensions={2,4,6}, to_apply=%region_16.0 | reduce | flops 229376 | bytes 1179652 | tf_op jit(solution)/shard_map/reduce_sum | solution.py:79
  473.2 7.9 %collective-permute-done.52 = f32[16,6,6,1]{3,0,2,1:T(8,128)S(1)} collective-permute-done((f32[16,6,6,1]{3,0,2,1:T(8,128)S(1)}, f32[16,6,6,1]{3,0,2,1:T(8,128)S(1)}, u32[]{:S(2)}, u32[]{:S(2)}) %collective-permute-start.52) | collective-permute-done | bytes 2336 | tf_op jit(solution)/shard_map/ppermute | solution.py:23
  481.0 5.1 collective-permute-done.53
  498.1 7.9 %collective-permute-done.58 = f32[16,6,6,1]{3,0,2,1:T(8,128)S(1)} collective-permute-done((f32[16,6,6,1]{3,0,2,1:T(8,128)S(1)}, f32[16,6,6,1]{3,0,2,1:T(8,128)S(1)}, u32[]{:S(2)}, u32[]{:S(2)}) %collective-permute-start.58) | collective-permute-done | bytes 2336 | tf_op jit(solution)/shard_map/ppermute | solution.py:23
  505.9 5.7 collective-permute-done.59
  524.5 7.9 %collective-permute-done.64 = f32[16,6,6,1]{3,0,2,1:T(8,128)S(1)} collective-permute-done((f32[16,6,6,1]{3,0,2,1:T(8,128)S(1)}, f32[16,6,6,1]{3,0,2,1:T(8,128)S(1)}, u32[]{:S(2)}, u32[]{:S(2)}) %collective-permute-start.64) | collective-permute-done | bytes 2336 | tf_op jit(solution)/shard_map/ppermute | solution.py:23
  532.4 5.5 collective-permute-done.65
  538.3 7.5 %broadcast_in_dim.5 = f32[16,4,2,4,2,128,2]{0,6,5,4,3,2,1:T(2,128)} broadcast(f32[16,4,4,128]{0,3,2,1:T(8,128)S(1)} %copy.767), dimensions={0,1,3,5} | broadcast | bytes 1179648 | tf_op jit(solution)/shard_map/broadcast_in_dim | solution.py:83
  545.8 6.1 %copy.768 = f32[16,8,8,256]{3,2,1,0:T(8,128)} copy(f32[16,8,8,256]{0,3,2,1:T(8,128)} %bitcast.137) | data formatting | bytes 2097152 | tf_op jit(solution)/shard_map/reshape | solution.py:83
  (284 shorter events, 273.1 us)
Async XLA Ops:
  1.8 6.7 %collective-permute-start = (f32[16,2,8,256]{3,2,1,0:T(8,128)S(1)}, f32[16,2,8,256]{3,2,1,0:T(8,128)S(1)}, u32[]{:S(2)}, u32[]{:S(2)}) collective-permute-start(f32[16,2,8,256]{3,2,1,0:T(8,128)S(1)} %get-tuple-element.72), channel_id=1, source_target_pairs={{0,8},{8,16},{16,24},{24,0},{1,9},{9,17},{17,25},{25,1},{2,10},{10... | collective-permute-start | bytes 786440 | tf_op jit(solution)/shard_map/ppermute | solution.py:23
  2.3 8.6 %collective-permute-start.1 = (f32[16,2,8,256]{3,2,1,0:T(8,128)S(1)}, f32[16,2,8,256]{3,2,1,0:T(8,128)S(1)}, u32[]{:S(2)}, u32[]{:S(2)}) collective-permute-start(f32[16,2,8,256]{3,2,1,0:T(8,128)S(1)} %get-tuple-element.71), channel_id=1, source_target_pairs={{8,0},{16,8},{24,16},{0,24},{9,1},{17,9},{25,17},{1,25},{10,2},{18... | collective-permute-start | bytes 786440 | tf_op jit(solution)/shard_map/ppermute | solution.py:26
  11.4 13.3 %collective-permute-start.3 = (f32[16,12,2,256]{3,0,2,1:T(8,128)S(1)}, f32[16,12,2,256]{3,0,2,1:T(8,128)S(1)}, u32[]{:S(2)}, u32[]{:S(2)}) collective-permute-start(f32[16,12,2,256]{3,0,2,1:T(8,128)S(1)} %copy.780), channel_id=1, source_target_pairs={{2,0},{4,2},{6,4},{0,6},{3,1},{5,3},{7,5},{1,7},{10,8},{12,10},{14... | collective-permute-start | bytes 1179656 | tf_op jit(solution)/shard_map/ppermute | solution.py:26
  15.3 18.4 %collective-permute-start.2 = (f32[16,12,2,256]{3,0,2,1:T(8,128)S(1)}, f32[16,12,2,256]{3,0,2,1:T(8,128)S(1)}, u32[]{:S(2)}, u32[]{:S(2)}) collective-permute-start(f32[16,12,2,256]{3,0,2,1:T(8,128)S(1)} %copy.779), channel_id=1, source_target_pairs={{0,2},{2,4},{4,6},{6,0},{1,3},{3,5},{5,7},{7,1},{8,10},{10,12},{12... | collective-permute-start | bytes 1179656 | tf_op jit(solution)/shard_map/ppermute | solution.py:23
  131.8 10.4 %collective-permute-start.9 = (f32[16,10,1,256]{3,0,2,1:T(8,128)S(1)}, f32[16,10,1,256]{3,0,2,1:T(8,128)S(1)}, u32[]{:S(2)}, u32[]{:S(2)}) collective-permute-start(f32[16,10,1,256]{3,0,2,1:T(8,128)S(1)} %copy.719), channel_id=1, source_target_pairs={{2,0},{4,2},{6,4},{0,6},{3,1},{5,3},{7,5},{1,7},{10,8},{12,10},{14... | collective-permute-start | bytes 491528 | tf_op jit(solution)/shard_map/ppermute | solution.py:26
  131.9 10.5 %collective-permute-start.8 = (f32[16,10,1,256]{3,0,2,1:T(8,128)S(1)}, f32[16,10,1,256]{3,0,2,1:T(8,128)S(1)}, u32[]{:S(2)}, u32[]{:S(2)}) collective-permute-start(f32[16,10,1,256]{3,0,2,1:T(8,128)S(1)} %copy.717), channel_id=1, source_target_pairs={{0,2},{2,4},{4,6},{6,0},{1,3},{3,5},{5,7},{7,1},{8,10},{10,12},{12... | collective-permute-start | bytes 491528 | tf_op jit(solution)/shard_map/ppermute | solution.py:23
  187.1 9.9 %collective-permute-start.16 = (f32[16,6,6,1]{3,0,2,1:T(8,128)S(1)}, f32[16,6,6,1]{3,0,2,1:T(8,128)S(1)}, u32[]{:S(2)}, u32[]{:S(2)}) collective-permute-start(f32[16,6,6,1]{3,0,2,1:T(8,128)S(1)} %get-tuple-element.83), channel_id=1, source_target_pairs={{0,1},{1,0},{2,3},{3,2},{4,5},{5,4},{6,7},{7,6},{8,9},{9,8},{10,11... | collective-permute-start | bytes 6920 | tf_op jit(solution)/shard_map/ppermute | solution.py:23
  187.9 15.2 %collective-permute-start.17 = (f32[16,6,6,1]{3,0,2,1:T(8,128)S(1)}, f32[16,6,6,1]{3,0,2,1:T(8,128)S(1)}, u32[]{:S(2)}, u32[]{:S(2)}) collective-permute-start(f32[16,6,6,1]{3,0,2,1:T(8,128)S(1)} %get-tuple-element.84), channel_id=1, source_target_pairs={{1,0},{0,1},{3,2},{2,3},{5,4},{4,5},{7,6},{6,7},{9,8},{8,9},{11,10... | collective-permute-start | bytes 6920 | tf_op jit(solution)/shard_map/ppermute | solution.py:26
  206.8 6.2 %collective-permute-start.20 = (f32[16,6,1,128]{3,0,2,1:T(8,128)S(1)}, f32[16,6,1,128]{3,0,2,1:T(8,128)S(1)}, u32[]{:S(2)}, u32[]{:S(2)}) collective-permute-start(f32[16,6,1,128]{3,0,2,1:T(8,128)S(1)} %get-tuple-element.97), channel_id=1, source_target_pairs={{0,2},{2,4},{4,6},{6,0},{1,3},{3,5},{5,7},{7,1},{8,10},{10,12},{12... | collective-permute-start | bytes 147464 | tf_op jit(solution)/shard_map/ppermute | solution.py:23
  213.2 9.9 %collective-permute-start.22 = (f32[16,6,6,1]{3,0,2,1:T(8,128)S(1)}, f32[16,6,6,1]{3,0,2,1:T(8,128)S(1)}, u32[]{:S(2)}, u32[]{:S(2)}) collective-permute-start(f32[16,6,6,1]{3,0,2,1:T(8,128)S(1)} %get-tuple-element.81), channel_id=1, source_target_pairs={{0,1},{1,0},{2,3},{3,2},{4,5},{5,4},{6,7},{7,6},{8,9},{9,8},{10,11... | collective-permute-start | bytes 6920 | tf_op jit(solution)/shard_map/ppermute | solution.py:23
  214.1 14.1 %collective-permute-start.23 = (f32[16,6,6,1]{3,0,2,1:T(8,128)S(1)}, f32[16,6,6,1]{3,0,2,1:T(8,128)S(1)}, u32[]{:S(2)}, u32[]{:S(2)}) collective-permute-start(f32[16,6,6,1]{3,0,2,1:T(8,128)S(1)} %get-tuple-element.82), channel_id=1, source_target_pairs={{1,0},{0,1},{3,2},{2,3},{5,4},{4,5},{7,6},{6,7},{9,8},{8,9},{11,10... | collective-permute-start | bytes 6920 | tf_op jit(solution)/shard_map/ppermute | solution.py:26
  231.8 6.2 %collective-permute-start.26 = (f32[16,6,1,128]{3,0,2,1:T(8,128)S(1)}, f32[16,6,1,128]{3,0,2,1:T(8,128)S(1)}, u32[]{:S(2)}, u32[]{:S(2)}) collective-permute-start(f32[16,6,1,128]{3,0,2,1:T(8,128)S(1)} %get-tuple-element.95), channel_id=1, source_target_pairs={{0,2},{2,4},{4,6},{6,0},{1,3},{3,5},{5,7},{7,1},{8,10},{10,12},{12... | collective-permute-start | bytes 147464 | tf_op jit(solution)/shard_map/ppermute | solution.py:23
  239.1 9.9 %collective-permute-start.28 = (f32[16,6,6,1]{3,0,2,1:T(8,128)S(1)}, f32[16,6,6,1]{3,0,2,1:T(8,128)S(1)}, u32[]{:S(2)}, u32[]{:S(2)}) collective-permute-start(f32[16,6,6,1]{3,0,2,1:T(8,128)S(1)} %get-tuple-element.79), channel_id=1, source_target_pairs={{0,1},{1,0},{2,3},{3,2},{4,5},{5,4},{6,7},{7,6},{8,9},{9,8},{10,11... | collective-permute-start | bytes 6920 | tf_op jit(solution)/shard_map/ppermute | solution.py:23
  240.0 14.1 %collective-permute-start.29 = (f32[16,6,6,1]{3,0,2,1:T(8,128)S(1)}, f32[16,6,6,1]{3,0,2,1:T(8,128)S(1)}, u32[]{:S(2)}, u32[]{:S(2)}) collective-permute-start(f32[16,6,6,1]{3,0,2,1:T(8,128)S(1)} %get-tuple-element.80), channel_id=1, source_target_pairs={{1,0},{0,1},{3,2},{2,3},{5,4},{4,5},{7,6},{6,7},{9,8},{8,9},{11,10... | collective-permute-start | bytes 6920 | tf_op jit(solution)/shard_map/ppermute | solution.py:26
  274.5 8.3 %collective-permute-start.33 = (f32[16,10,1,256]{3,0,2,1:T(8,128)S(1)}, f32[16,10,1,256]{3,0,2,1:T(8,128)S(1)}, u32[]{:S(2)}, u32[]{:S(2)}) collective-permute-start(f32[16,10,1,256]{3,0,2,1:T(8,128)S(1)} %copy.735), channel_id=1, source_target_pairs={{2,0},{4,2},{6,4},{0,6},{3,1},{5,3},{7,5},{1,7},{10,8},{12,10},{14... | collective-permute-start | bytes 491528 | tf_op jit(solution)/shard_map/ppermute | solution.py:26
  278.1 8.6 %collective-permute-start.32 = (f32[16,10,1,256]{3,0,2,1:T(8,128)S(1)}, f32[16,10,1,256]{3,0,2,1:T(8,128)S(1)}, u32[]{:S(2)}, u32[]{:S(2)}) collective-permute-start(f32[16,10,1,256]{3,0,2,1:T(8,128)S(1)} %copy.733), channel_id=1, source_target_pairs={{0,2},{2,4},{4,6},{6,0},{1,3},{3,5},{5,7},{7,1},{8,10},{10,12},{12... | collective-permute-start | bytes 491528 | tf_op jit(solution)/shard_map/ppermute | solution.py:23
  307.0 7.4 %collective-permute-start.36 = (f32[16,2,8,256]{3,2,1,0:T(8,128)S(1)}, f32[16,2,8,256]{3,2,1,0:T(8,128)S(1)}, u32[]{:S(2)}, u32[]{:S(2)}) collective-permute-start(f32[16,2,8,256]{3,2,1,0:T(8,128)S(1)} %get-tuple-element.62), channel_id=1, source_target_pairs={{0,8},{8,16},{16,24},{24,0},{1,9},{9,17},{17,25},{25,1},{2,10},{10... | collective-permute-start | bytes 786440 | tf_op jit(solution)/shard_map/ppermute | solution.py:23
  307.0 7.4 %collective-permute-start.37 = (f32[16,2,8,256]{3,2,1,0:T(8,128)S(1)}, f32[16,2,8,256]{3,2,1,0:T(8,128)S(1)}, u32[]{:S(2)}, u32[]{:S(2)}) collective-permute-start(f32[16,2,8,256]{3,2,1,0:T(8,128)S(1)} %get-tuple-element.63), channel_id=1, source_target_pairs={{8,0},{16,8},{24,16},{0,24},{9,1},{17,9},{25,17},{1,25},{10,2},{18... | collective-permute-start | bytes 786440 | tf_op jit(solution)/shard_map/ppermute | solution.py:26
  314.8 12.4 %collective-permute-start.39 = (f32[16,12,2,256]{3,0,2,1:T(8,128)S(1)}, f32[16,12,2,256]{3,0,2,1:T(8,128)S(1)}, u32[]{:S(2)}, u32[]{:S(2)}) collective-permute-start(f32[16,12,2,256]{3,0,2,1:T(8,128)S(1)} %copy.745), channel_id=1, source_target_pairs={{2,0},{4,2},{6,4},{0,6},{3,1},{5,3},{7,5},{1,7},{10,8},{12,10},{14... | collective-permute-start | bytes 1179656 | tf_op jit(solution)/shard_map/ppermute | solution.py:26
  317.4 18.3 %collective-permute-start.38 = (f32[16,12,2,256]{3,0,2,1:T(8,128)S(1)}, f32[16,12,2,256]{3,0,2,1:T(8,128)S(1)}, u32[]{:S(2)}, u32[]{:S(2)}) collective-permute-start(f32[16,12,2,256]{3,0,2,1:T(8,128)S(1)} %copy.743), channel_id=1, source_target_pairs={{0,2},{2,4},{4,6},{6,0},{1,3},{3,5},{5,7},{7,1},{8,10},{10,12},{12... | collective-permute-start | bytes 1179656 | tf_op jit(solution)/shard_map/ppermute | solution.py:23
  413.5 6.9 %collective-permute-start.45 = (f32[16,10,1,256]{3,0,2,1:T(8,128)S(1)}, f32[16,10,1,256]{3,0,2,1:T(8,128)S(1)}, u32[]{:S(2)}, u32[]{:S(2)}) collective-permute-start(f32[16,10,1,256]{3,0,2,1:T(8,128)S(1)} %copy.755), channel_id=1, source_target_pairs={{2,0},{4,2},{6,4},{0,6},{3,1},{5,3},{7,5},{1,7},{10,8},{12,10},{14... | collective-permute-start | bytes 491528 | tf_op jit(solution)/shard_map/ppermute | solution.py:26
  415.9 9.1 %collective-permute-start.44 = (f32[16,10,1,256]{3,0,2,1:T(8,128)S(1)}, f32[16,10,1,256]{3,0,2,1:T(8,128)S(1)}, u32[]{:S(2)}, u32[]{:S(2)}) collective-permute-start(f32[16,10,1,256]{3,0,2,1:T(8,128)S(1)} %copy.753), channel_id=1, source_target_pairs={{0,2},{2,4},{4,6},{6,0},{1,3},{3,5},{5,7},{7,1},{8,10},{10,12},{12... | collective-permute-start | bytes 491528 | tf_op jit(solution)/shard_map/ppermute | solution.py:23
  463.8 6.5 %collective-permute-start.50 = (f32[16,6,1,128]{3,0,2,1:T(8,128)S(1)}, f32[16,6,1,128]{3,0,2,1:T(8,128)S(1)}, u32[]{:S(2)}, u32[]{:S(2)}) collective-permute-start(f32[16,6,1,128]{3,0,2,1:T(8,128)S(1)} %get-tuple-element.93), channel_id=1, source_target_pairs={{0,2},{2,4},{4,6},{6,0},{1,3},{3,5},{5,7},{7,1},{8,10},{10,12},{12... | collective-permute-start | bytes 147464 | tf_op jit(solution)/shard_map/ppermute | solution.py:23
  471.1 9.9 %collective-permute-start.52 = (f32[16,6,6,1]{3,0,2,1:T(8,128)S(1)}, f32[16,6,6,1]{3,0,2,1:T(8,128)S(1)}, u32[]{:S(2)}, u32[]{:S(2)}) collective-permute-start(f32[16,6,6,1]{3,0,2,1:T(8,128)S(1)} %get-tuple-element.77), channel_id=1, source_target_pairs={{0,1},{1,0},{2,3},{3,2},{4,5},{5,4},{6,7},{7,6},{8,9},{9,8},{10,11... | collective-permute-start | bytes 6920 | tf_op jit(solution)/shard_map/ppermute | solution.py:23
  471.5 14.6 %collective-permute-start.53 = (f32[16,6,6,1]{3,0,2,1:T(8,128)S(1)}, f32[16,6,6,1]{3,0,2,1:T(8,128)S(1)}, u32[]{:S(2)}, u32[]{:S(2)}) collective-permute-start(f32[16,6,6,1]{3,0,2,1:T(8,128)S(1)} %get-tuple-element.78), channel_id=1, source_target_pairs={{1,0},{0,1},{3,2},{2,3},{5,4},{4,5},{7,6},{6,7},{9,8},{8,9},{11,10... | collective-permute-start | bytes 6920 | tf_op jit(solution)/shard_map/ppermute | solution.py:26
  496.0 9.9 %collective-permute-start.58 = (f32[16,6,6,1]{3,0,2,1:T(8,128)S(1)}, f32[16,6,6,1]{3,0,2,1:T(8,128)S(1)}, u32[]{:S(2)}, u32[]{:S(2)}) collective-permute-start(f32[16,6,6,1]{3,0,2,1:T(8,128)S(1)} %get-tuple-element.75), channel_id=1, source_target_pairs={{0,1},{1,0},{2,3},{3,2},{4,5},{5,4},{6,7},{7,6},{8,9},{9,8},{10,11... | collective-permute-start | bytes 6920 | tf_op jit(solution)/shard_map/ppermute | solution.py:23
  497.4 14.2 %collective-permute-start.59 = (f32[16,6,6,1]{3,0,2,1:T(8,128)S(1)}, f32[16,6,6,1]{3,0,2,1:T(8,128)S(1)}, u32[]{:S(2)}, u32[]{:S(2)}) collective-permute-start(f32[16,6,6,1]{3,0,2,1:T(8,128)S(1)} %get-tuple-element.76), channel_id=1, source_target_pairs={{1,0},{0,1},{3,2},{2,3},{5,4},{4,5},{7,6},{6,7},{9,8},{8,9},{11,10... | collective-permute-start | bytes 6920 | tf_op jit(solution)/shard_map/ppermute | solution.py:26
  515.2 6.3 %collective-permute-start.62 = (f32[16,6,1,128]{3,0,2,1:T(8,128)S(1)}, f32[16,6,1,128]{3,0,2,1:T(8,128)S(1)}, u32[]{:S(2)}, u32[]{:S(2)}) collective-permute-start(f32[16,6,1,128]{3,0,2,1:T(8,128)S(1)} %get-tuple-element.89), channel_id=1, source_target_pairs={{0,2},{2,4},{4,6},{6,0},{1,3},{3,5},{5,7},{7,1},{8,10},{10,12},{12... | collective-permute-start | bytes 147464 | tf_op jit(solution)/shard_map/ppermute | solution.py:23
  522.4 9.9 %collective-permute-start.64 = (f32[16,6,6,1]{3,0,2,1:T(8,128)S(1)}, f32[16,6,6,1]{3,0,2,1:T(8,128)S(1)}, u32[]{:S(2)}, u32[]{:S(2)}) collective-permute-start(f32[16,6,6,1]{3,0,2,1:T(8,128)S(1)} %get-tuple-element.73), channel_id=1, source_target_pairs={{0,1},{1,0},{2,3},{3,2},{4,5},{5,4},{6,7},{7,6},{8,9},{9,8},{10,11... | collective-permute-start | bytes 6920 | tf_op jit(solution)/shard_map/ppermute | solution.py:23
  523.1 14.7 %collective-permute-start.65 = (f32[16,6,6,1]{3,0,2,1:T(8,128)S(1)}, f32[16,6,6,1]{3,0,2,1:T(8,128)S(1)}, u32[]{:S(2)}, u32[]{:S(2)}) collective-permute-start(f32[16,6,6,1]{3,0,2,1:T(8,128)S(1)} %get-tuple-element.74), channel_id=1, source_target_pairs={{1,0},{0,1},{3,2},{2,3},{5,4},{4,5},{7,6},{6,7},{9,8},{8,9},{11,10... | collective-permute-start | bytes 6920 | tf_op jit(solution)/shard_map/ppermute | solution.py:26
  559.0 7.0 %collective-permute-start.69 = (f32[16,10,1,256]{3,0,2,1:T(8,128)S(1)}, f32[16,10,1,256]{3,0,2,1:T(8,128)S(1)}, u32[]{:S(2)}, u32[]{:S(2)}) collective-permute-start(f32[16,10,1,256]{3,0,2,1:T(8,128)S(1)} %copy.771), channel_id=1, source_target_pairs={{2,0},{4,2},{6,4},{0,6},{3,1},{5,3},{7,5},{1,7},{10,8},{12,10},{14... | collective-permute-start | bytes 491528 | tf_op jit(solution)/shard_map/ppermute | solution.py:26
  561.6 8.9 %collective-permute-start.68 = (f32[16,10,1,256]{3,0,2,1:T(8,128)S(1)}, f32[16,10,1,256]{3,0,2,1:T(8,128)S(1)}, u32[]{:S(2)}, u32[]{:S(2)}) collective-permute-start(f32[16,10,1,256]{3,0,2,1:T(8,128)S(1)} %copy.769), channel_id=1, source_target_pairs={{0,2},{2,4},{4,6},{6,0},{1,3},{3,5},{5,7},{7,1},{8,10},{10,12},{12... | collective-permute-start | bytes 491528 | tf_op jit(solution)/shard_map/ppermute | solution.py:23
  (58 other events, 391.7 us)
